TPU v7x, 32 devices: a whole 2x2x4 slice. The times are simulated.
32 devices in a mesh: grp: 2 (over y), bn: 16 (over z, x, core).
Axes of the slice: x: 2, y: 2, z: 4, core: 2. Of those that a mesh axis runs over, the one named last changes fastest.
Arguments:
- images: bfloat16 [32, 19, 19, 384], P(('grp', 'bn')), parts along dimension 0, may hold values from -56 to 56
- expand_weight: bfloat16 [384, 2304], P('bn'), may hold values from -0.3125 to 0.3125
- expand_gain: float32 [2304], replicated, may hold values from 0.5 to 2
- expand_shift: float32 [2304], replicated, may hold values from -3 to 3
- depth_weight: bfloat16 [25, 2304], replicated, may hold values from -1.25 to 1.25
- depth_gain: float32 [2304], replicated, may hold values from 0.5 to 2
- depth_shift: float32 [2304], replicated, may hold values from -3 to 3
- squeeze_weight: bfloat16 [2304, 96], replicated, may hold values from -0.125 to 0.125
- squeeze_bias: float32 [96], replicated, may hold values from -4 to 4
- excite_weight: bfloat16 [96, 2304], replicated, may hold values from -0.625 to 0.625
- excite_bias: float32 [2304], replicated, may hold values from -4 to 4
- project_weight: bfloat16 [2304, 384], P('bn'), may hold values from -0.125 to 0.125
- project_gain: float32 [384], replicated, may hold values from 0.5 to 2
- project_shift: float32 [384], replicated, may hold values from -3 to 3
- group_table: int32 [32], P('grp'), parts along dimension 0, may hold values from 0 to 1, as said below
Outputs:
- block_output: bfloat16 [32, 19, 19, 384], P(('grp', 'bn')), parts along dimension 0
There are 2 independent parts, one for each index of `grp`. A program takes and returns all parts, laid end to end along the dimension named above; an argument that names none is the same for every part. Nothing has to cross between parts.
Inputs may be any that keep to these rules, and one draw needn't show every extreme that they name: `group_table`: each of the 2 statistics groups holds at least 4 images, placed anywhere among the images.
All inputs are finite; a program needn't handle non-finite values.
Results may differ from a plain program's by a relative error of at most 0.0065.
Values may be sent and summed in bfloat16 or wider, within the bound.
A program may use at most 64 MiB of HBM per device.

v0:
```python
import jax
import jax.numpy as jnp
from jax import lax
from jax.sharding import PartitionSpec as P

KERNEL = 5
STAT_GROUPS = 2
epsilon = 0.001


def normalize(values, centre, inverse, gain, shift):
    return (values.astype(jnp.float32) - centre) * inverse * gain + shift


def depthwise(widened, depth_weight, height, breadth):
    spatial = widened.reshape(height, breadth, widened.shape[-1])
    margin = KERNEL // 2
    padded = jnp.pad(spatial, ((margin, margin), (margin, margin), (0, 0)))
    accumulated = jnp.zeros(spatial.shape, jnp.float32)
    for row_shift in range(KERNEL):
        for col_shift in range(KERNEL):
            window = padded[row_shift : row_shift + height, col_shift : col_shift + breadth]
            accumulated = accumulated + window.astype(jnp.float32) * depth_weight[
                row_shift * KERNEL + col_shift
            ].astype(jnp.float32)
    return accumulated.reshape(height * breadth, spatial.shape[-1]).astype(jnp.bfloat16)


def group_moments(values, selector, population):
    totals = jnp.sum(values, axis=0, dtype=jnp.float32)
    squares = jnp.sum(jnp.square(values.astype(jnp.float32)), axis=0)
    weighted = selector[:, None, None] * jnp.stack([totals, squares])[None]
    summed = lax.psum(weighted, "bn")
    picked = jnp.sum(selector[:, None, None] * summed, axis=0)
    centre = picked[0] / population
    spread = picked[1] / population - centre * centre
    return (centre, lax.rsqrt(spread + epsilon))


def on_device(
    images,
    expand_weight,
    expand_gain,
    expand_shift,
    depth_weight,
    depth_gain,
    depth_shift,
    squeeze_weight,
    squeeze_bias,
    excite_weight,
    excite_bias,
    project_weight,
    project_gain,
    project_shift,
    group_table,
):
    height, breadth, channels = (images.shape[1], images.shape[2], images.shape[3])
    pixels = height * breadth
    flattened = images.reshape(pixels, channels)
    device_rank = lax.axis_index("bn")
    ranks_all = jnp.arange(group_table.shape[0], dtype=jnp.int32)
    my_group = jnp.sum(jnp.where(ranks_all == device_rank, group_table, 0))
    members = jnp.sum((group_table == my_group).astype(jnp.float32))
    population = members * pixels
    selector = (jnp.arange(STAT_GROUPS, dtype=jnp.int32) == my_group).astype(jnp.float32)
    inputs = flattened
    expanded = jnp.dot(
        inputs,
        lax.all_gather(expand_weight, "bn", axis=0, tiled=True),
        preferred_element_type=jnp.float32,
    ).astype(jnp.bfloat16)
    centre, inverse = group_moments(expanded, selector, population)
    widened = jax.nn.silu(normalize(expanded, centre, inverse, expand_gain, expand_shift)).astype(
        jnp.bfloat16
    )
    filtered = depthwise(widened, depth_weight, height, breadth)
    centre, inverse = group_moments(filtered, selector, population)
    activated = jax.nn.silu(normalize(filtered, centre, inverse, depth_gain, depth_shift)).astype(
        jnp.bfloat16
    )
    pooled = (jnp.sum(activated, axis=0, dtype=jnp.float32) / pixels).astype(jnp.bfloat16)[None, :]
    squeezed = jax.nn.silu(
        jnp.dot(pooled, squeeze_weight, preferred_element_type=jnp.float32) + squeeze_bias
    ).astype(jnp.bfloat16)
    excitation = jax.nn.sigmoid(
        jnp.dot(squeezed, excite_weight, preferred_element_type=jnp.float32) + excite_bias
    )
    gated_input = (activated * excitation).astype(jnp.bfloat16)
    inputs = gated_input
    projected = jnp.dot(
        inputs,
        lax.all_gather(project_weight, "bn", axis=0, tiled=True),
        preferred_element_type=jnp.float32,
    ).astype(jnp.bfloat16)
    centre, inverse = group_moments(projected, selector, population)
    output = flattened.astype(jnp.float32) + normalize(
        projected, centre, inverse, project_gain, project_shift
    )
    return output.astype(jnp.bfloat16).reshape(images.shape)


def solution(mesh):
    return jax.shard_map(
        on_device,
        mesh=mesh,
        in_specs=(
            P(("grp", "bn"), None, None, None),
            P("bn", None),
            P(),
            P(),
            P(),
            P(),
            P(),
            P(),
            P(),
            P(),
            P(),
            P("bn", None),
            P(),
            P(),
            P("grp"),
        ),
        out_specs=P(("grp", "bn"), None, None, None),
        check_vma=False,
    )
```

profile of v0, /device:TPU:0, one launch (start us, length us, event | category | flops | bytes accessed | tf_op | source)
XLA Modules:
  0.0 257.8 jit_solution(15007953222312947867)
XLA Ops:
  6.5 0.0 copy-start
  6.5 0.0 all-gather.3.cloned.1.call-start
  6.5 0.7 all-gather.3.cloned.1.call-update
  7.3 0.0 all-gather.5.cloned.1.call-start
  7.3 0.7 all-gather.5.cloned.1.call-update
  8.0 1.3 fusion.15
  9.3 0.6 compare_convert_fusion.1
  10.0 1.9 fusion.16
  11.9 1.9 convert_reduce_fusion.27
  13.7 1.1 convert_reduce_fusion.26
  14.9 1.1 reshape.239
  16.5 0.0 copy-start.2
  16.5 0.0 copy-start.3
  16.6 36.0 %all-gather.3.cloned.1.call-done = bf16[384,2304]{1,0:T(8,128)(2,1)} async-done(((bf16[24,2304]{1,0:T(8,128)(2,1)}), bf16[384,2304]{1,0:T(8,128)(2,1)}) %all-gather.3.cloned.1.call-update) | async-done | bytes 1769488 | tf_op jit(solution)/shard_map/all_gather | solution.py:69
  52.5 3.7 %convert_reduce_fusion = (f32[2304]{0:T(1024)S(1)}, f32[2304]{0:T(1024)S(1)}, bf16[361,2304]{1,0:T(8,128)(2,1)}) fusion(bf16[361,384]{1,0:T(8,128)(2,1)S(1)} %reshape.239, bf16[384,2304]{1,0:T(8,128)(2,1)} %all-gather.3.cloned.1.call-done), kind=kOutput, calls=%fused_computation.2 | convolution fusion | flops 642933504 | bytes 3728640 | tf_op jit(solution)/shard_map/dot_general | solution.py:67
  56.3 0.1 broadcast_multiply_fusion.1
  56.4 59.8 %psum.21 = f32[2,2,2304]{2,1,0:T(2,128)S(1)} all-reduce(f32[2,2,2304]{2,1,0:T(2,128)S(1)} %broadcast_multiply_fusion.1), channel_id=1, replica_groups=mesh['grp'=2,'bn'=16] {'bn'}, use_global_device_ids=true, to_apply=%region_3.4 | all-reduce | flops 9216 | bytes 73728 | tf_op jit(solution)/shard_map/psum | solution.py:33
  116.2 0.1 multiply_reduce_fusion.3
  116.3 0.1 fusion.26
  116.3 0.0 copy-done.2
  116.4 0.0 copy-done.3
  116.4 2.6 %fusion.9 = bf16[361,2304]{1,0:T(8,128)(2,1)S(1)} fusion(bf16[361,2304]{1,0:T(8,128)(2,1)} %get-tuple-element.43, f32[2304]{0:T(1024)S(1)} %copy-done.2, f32[2304]{0:T(1024)S(1)} %copy-done.3, f32[2304]{0:T(1024)S(1)} %get-tuple-element.39, f32[2304]{0:T(1024)S(1)} %get-tuple-element.38), kind=kLoop, calls=%fused_computation.17 | loop fusion | flops 8317440 | bytes 3363840 | tf_op jit(solution)/shard_map/convert_element_type | solution.py:73
  119.0 2.0 reshape.240
  121.0 32.3 %convert_reduce_fusion.2 = (f32[2304]{0:T(1024)S(1)}, f32[2304]{0:T(1024)S(1)}, bf16[19,19,2304]{2,1,0:T(8,128)(2,1)S(1)}) fusion(f32[2304]{0:T(1024)S(1)} %get-tuple-element.34, f32[2304]{0:T(1024)S(1)} %get-tuple-element.35, f32[2304]{0:T(1024)S(1)} %get-tuple-element.12, f32[2304]{0:T(1024)S(1)} %get-tuple-element.13, f32[2304]{0:T(1024)S(1)} %get-tuple-element.14, ...), kind=kLoop, calls=%fused_computation.20 | loop fusion | flops 65703168 | bytes 3575808 | tf_op jit(solution)/shard_map/reduce_sum | solution.py:30
  153.3 0.0 copy-start.4
  153.3 0.0 copy-start.5
  153.3 0.0 copy-start.1
  153.3 0.0 copy-start.9
  153.4 0.0 copy-start.6
  153.4 2.2 reshape.267
  155.6 0.1 broadcast_multiply_fusion
  155.7 57.9 %psum.22 = f32[2,2,2304]{2,1,0:T(2,128)S(1)} all-reduce(f32[2,2,2304]{2,1,0:T(2,128)S(1)} %broadcast_multiply_fusion), channel_id=1, replica_groups=mesh['grp'=2,'bn'=16] {'bn'}, use_global_device_ids=true, to_apply=%region_8.9 | all-reduce | flops 9216 | bytes 73728 | tf_op jit(solution)/shard_map/psum | solution.py:33
  213.6 0.1 multiply_reduce_fusion.2
  213.7 0.1 fusion.25
  213.7 0.0 copy-done.4
  213.8 1.6 convert_reduce_fusion.1
  215.4 0.4 convolution_reduce_fusion
  215.8 0.0 copy-done.6
  215.8 0.0 copy-start.7
  215.8 0.0 copy-start.8
  215.9 0.0 all-gather.5.cloned.1.call-done
  215.9 3.9 %fusion.24 = (f32[384]{0:T(512)S(1)}, f32[384]{0:T(512)S(1)}, f32[361,384]{1,0:T(8,128)S(1)}) fusion(bf16[2304,384]{1,0:T(8,128)(2,1)} %all-gather.5.cloned.1.call-done, f32[2304]{0:T(1024)S(1)} %add_divide_fusion, f32[2304]{0:T(1024)S(1)} %copy-done.4, f32[2304]{0:T(1024)S(1)} %copy-done.5, f32[2304]{0:T(1024)S(1)} %get-tuple-element.37, ...), kind=kOutput, calls=%fused_computation.106 | convolution fusion | flops 649452672 | bytes 5700096 | tf_op jit(solution)/shard_map/dot_general | solution.py:90
  219.8 0.1 broadcast_multiply_fusion.2
  219.9 30.0 %psum.23 = f32[2,2,384]{2,1,0:T(2,128)S(1)} all-reduce(f32[2,2,384]{2,1,0:T(2,128)S(1)} %broadcast_multiply_fusion.2), channel_id=1, replica_groups=mesh['grp'=2,'bn'=16] {'bn'}, use_global_device_ids=true, to_apply=%region_13.14 | all-reduce | flops 1536 | bytes 12288 | tf_op jit(solution)/shard_map/psum | solution.py:33
  249.9 0.1 multiply_reduce_fusion.4
  250.0 0.0 copy-done.8
  250.0 0.1 add_convert_fusion.1
  250.2 0.8 reshape.241
  (18 shorter events, 0.2 us)
Async XLA Ops:
  6.5 208.8 %copy-start = (bf16[96,2304]{1,0:T(8,128)(2,1)S(1)}, bf16[96,2304]{1,0:T(8,128)(2,1)}, u32[]{:S(2)}) copy-start(bf16[96,2304]{1,0:T(8,128)(2,1)} %param.24) | copy-start | bytes 1327108
  6.5 46.0 %all-gather.3.cloned.1.call-start = ((), (), s32[]{:S(2)}) async-start(), calls=%async_computation | async-start | bytes 1880064 | tf_op jit(solution)/shard_map/all_gather | solution.py:69
  7.3 208.6 %all-gather.5.cloned.1.call-start = ((), (), s32[]{:S(2)}) async-start(), calls=%async_computation.1 | async-start | bytes 1880064 | tf_op jit(solution)/shard_map/all_gather | solution.py:92
  16.5 99.8 %copy-start.2 = (f32[2304]{0:T(1024)S(1)}, f32[2304]{0:T(1024)}, u32[]{:S(2)}) copy-start(f32[2304]{0:T(1024)} %param.18) | copy-start | bytes 27652
  16.5 99.8 %copy-start.3 = (f32[2304]{0:T(1024)S(1)}, f32[2304]{0:T(1024)}, u32[]{:S(2)}) copy-start(f32[2304]{0:T(1024)} %param.17) | copy-start | bytes 27652
  153.3 60.4 %copy-start.4 = (f32[2304]{0:T(1024)S(1)}, f32[2304]{0:T(1024)}, u32[]{:S(2)}) copy-start(f32[2304]{0:T(1024)} %param.21) | copy-start | bytes 27652
  153.3 60.4 %copy-start.5 = (f32[2304]{0:T(1024)S(1)}, f32[2304]{0:T(1024)}, u32[]{:S(2)}) copy-start(f32[2304]{0:T(1024)} %param.20) | copy-start | bytes 27652
  153.3 62.0 %copy-start.1 = (bf16[2304,96]{0,1:T(8,128)(2,1)S(1)}, bf16[2304,96]{0,1:T(8,128)(2,1)}, u32[]{:S(2)}) copy-start(bf16[2304,96]{0,1:T(8,128)(2,1)} %param.22) | copy-start | bytes 1327108
  153.3 62.0 %copy-start.9 = (f32[96]{0:T(128)S(1)}, f32[96]{0:T(128)}, u32[]{:S(2)}) copy-start(f32[96]{0:T(128)} %param.23) | copy-start | bytes 1156
  153.4 62.5 %copy-start.6 = (f32[2304]{0:T(1024)S(1)}, f32[2304]{0:T(1024)}, u32[]{:S(2)}) copy-start(f32[2304]{0:T(1024)} %param.25) | copy-start | bytes 27652
  215.8 34.2 %copy-start.7 = (f32[384]{0:T(512)S(1)}, f32[384]{0:T(512)}, u32[]{:S(2)}) copy-start(f32[384]{0:T(512)} %param.28) | copy-start | bytes 4612
  215.8 34.2 %copy-start.8 = (f32[384]{0:T(512)S(1)}, f32[384]{0:T(512)}, u32[]{:S(2)}) copy-start(f32[384]{0:T(512)} %param.27) | copy-start | bytes 4612
Sparse Core Ops, SparseCore 0:
  9.5 42.9 all-gather.2
  54.7 39.2 all-gather.4
where the time goes:
time: 258 us
  blocking collectives  148 us (57%)
  other arithmetic  44.2 us (17%)
  waiting for transfers between devices  37.4 us (14%)
  between operations  14.3 us (6%)
  matrix products  8.06 us (3%)
  local copies, waits for them, and re-layouts  6.24 us (2%)
    psum x3, blocking collectives, group_moments(): summed = lax.psum(weighted, 'bn')  148 us
    all_gather x1, waiting for transfers between devices, on_device(): lax.all_gather(expand_weight, 'bn', axis=0, tiled=True)  36 us
    reduce_sum x1, other arithmetic, group_moments(): totals = jnp.sum(values, axis=0, dtype=jnp.float32)  32.3 us
  transfers between devices with their start and end apart: 2, of which 1 were waited for; matrix products, arithmetic and copies ran while one was open for 21% of the time, Pallas kernels for 0%

commit v1 on v0

--- a/solution.py
+++ b/solution.py
@@ -66,7 +66,9 @@
     inputs = flattened
     expanded = jnp.dot(
         inputs,
-        lax.all_gather(expand_weight, "bn", axis=0, tiled=True),
+        jnp.concatenate(
+            lax.all_to_all(jnp.stack([expand_weight] * lax.axis_size("bn")), "bn", 0, 0), axis=0
+        ),
         preferred_element_type=jnp.float32,
     ).astype(jnp.bfloat16)
     centre, inverse = group_moments(expanded, selector, population)

time: 258 us -> 270 us (1.047)
  blocking collectives: 148 us -> 158 us
  starting transfers between devices: 0.04 us -> 7.43 us
  other arithmetic: 44.2 us -> 41.2 us
    all_gather x1 -> x0, waiting for transfers between devices: 36 us -> none  [on_device(): lax.all_gather(expand_weight, 'bn', axis=0, tiled=True)]
    all_to_all x0 -> x1, waiting for transfers between devices: none -> 34.1 us  [on_device(): lax.all_to_all(jnp.stack([expand_weight] * lax.axis_size('bn')), 'bn', 0, 0)]
    psum x3, blocking collectives: 148 us -> 158 us  [group_moments(): summed = lax.psum(weighted, 'bn')]
    all_to_all x0 -> x1, starting transfers between devices: none -> 7.39 us  [on_device(): lax.all_to_all(jnp.stack([expand_weight] * lax.axis_size('bn')), 'bn', 0, 0)]
  transfers between devices with their start and end apart: 2 -> 2, of which waited for: 1 -> 1; matrix products, arithmetic and copies ran while one was open for 21% -> 18% of each run, Pallas kernels for 0% -> 0%
where the time goes in v1:
time: 270 us
  blocking collectives  158 us (59%)
  other arithmetic  41.2 us (15%)
  waiting for transfers between devices  34.8 us (13%)
  between operations  14.4 us (5%)
  local copies, waits for them, and re-layouts  7.53 us (3%)
  starting transfers between devices  7.43 us (3%)
  matrix products  6.58 us (2%)
    psum x3, blocking collectives, group_moments(): summed = lax.psum(weighted, 'bn')  158 us
    all_to_all x1, waiting for transfers between devices, on_device(): lax.all_to_all(jnp.stack([expand_weight] * lax.axis_size('bn')), 'bn', 0, 0)  34.1 us
    reduce_sum x1, other arithmetic, group_moments(): totals = jnp.sum(values, axis=0, dtype=jnp.float32)  33 us
    all_to_all x1, starting transfers between devices, on_device(): lax.all_to_all(jnp.stack([expand_weight] * lax.axis_size('bn')), 'bn', 0, 0)  7.39 us
  transfers between devices with their start and end apart: 2, of which 1 were waited for; matrix products, arithmetic and copies ran while one was open for 18% of the time, Pallas kernels for 0%

profile of v1, /device:TPU:0, one launch (start us, length us, event | category | flops | bytes accessed | tf_op | source)
XLA Modules:
  0.0 269.6 jit_solution(13897279232707616513)
XLA Ops:
  6.5 0.0 copy-start
  6.5 2.3 stack.20
  8.9 7.4 %all-to-all-start = ((bf16[16,24,2304]{2,1,0:T(8,128)(2,1)}), bf16[16,24,2304]{2,1,0:T(8,128)(2,1)S(1)}, u32[]{:S(2)}, u32[]{:S(2)}) async-start(bf16[16,24,2304]{2,1,0:T(8,128)(2,1)} %stack.20), calls=%async_computation | async-start | bytes 3538944 | tf_op jit(solution)/shard_map/all_to_all | solution.py:70
  16.2 0.0 all-gather.2.cloned.1.call-start
  16.3 0.7 all-gather.2.cloned.1.call-update
  17.0 0.0 copy-done.3
  17.0 0.1 reshape.244
  17.1 0.0 copy-done.12
  17.1 0.6 fusion.15
  17.8 1.3 fusion.16
  19.7 0.7 compare_convert_fusion.1
  20.3 0.0 copy-done.2
  20.3 0.2 convert_reduce_fusion.26
  20.5 0.5 convert_reduce_fusion.27
  21.0 34.1 %all-to-all-done = bf16[16,24,2304]{2,1,0:T(8,128)(2,1)S(1)} async-done(((bf16[16,24,2304]{2,1,0:T(8,128)(2,1)}), bf16[16,24,2304]{2,1,0:T(8,128)(2,1)S(1)}, u32[]{:S(2)}, u32[]{:S(2)}) %all-to-all-start) | async-done | bytes 1769504 | tf_op jit(solution)/shard_map/all_to_all | solution.py:70
  55.1 2.3 convert_reduce_fusion
  57.4 0.1 broadcast_multiply_fusion.1
  57.5 69.8 %psum.21 = f32[2,2,2304]{2,1,0:T(2,128)S(1)} all-reduce(f32[2,2,2304]{2,1,0:T(2,128)S(1)} %broadcast_multiply_fusion.1), channel_id=1, replica_groups=mesh['grp'=2,'bn'=16] {'bn'}, use_global_device_ids=true, to_apply=%region_3.4 | all-reduce | flops 9216 | bytes 73728 | tf_op jit(solution)/shard_map/psum | solution.py:33
  127.3 0.1 multiply_reduce_fusion.3
  127.4 0.1 fusion.26
  127.5 0.0 copy-done.4
  127.5 0.0 copy-done.5
  127.5 2.6 fusion.9
  130.1 2.0 reshape.246
  132.1 33.0 %convert_reduce_fusion.2 = (f32[2304]{0:T(1024)S(1)}, f32[2304]{0:T(1024)S(1)}, bf16[19,19,2304]{2,1,0:T(8,128)(2,1)S(1)}) fusion(f32[2304]{0:T(1024)S(1)} %get-tuple-element.34, f32[2304]{0:T(1024)S(1)} %get-tuple-element.35, f32[2304]{0:T(1024)S(1)} %get-tuple-element.12, f32[2304]{0:T(1024)S(1)} %get-tuple-element.13, f32[2304]{0:T(1024)S(1)} %get-tuple-element.14, ...), kind=kLoop, calls=%fused_computation.20 | loop fusion | flops 65703168 | bytes 3575808 | tf_op jit(solution)/shard_map/reduce_sum | solution.py:30
  165.1 0.0 copy-start.6
  165.1 0.0 copy-start.7
  165.1 0.0 copy-start.1
  165.1 0.0 copy-start.11
  165.1 0.0 copy-start.8
  165.2 2.2 reshape.273
  167.4 0.1 broadcast_multiply_fusion
  167.5 57.9 %psum.22 = f32[2,2,2304]{2,1,0:T(2,128)S(1)} all-reduce(f32[2,2,2304]{2,1,0:T(2,128)S(1)} %broadcast_multiply_fusion), channel_id=1, replica_groups=mesh['grp'=2,'bn'=16] {'bn'}, use_global_device_ids=true, to_apply=%region_8.9 | all-reduce | flops 9216 | bytes 73728 | tf_op jit(solution)/shard_map/psum | solution.py:33
  225.3 0.1 multiply_reduce_fusion.2
  225.4 0.1 fusion.25
  225.5 0.0 copy-done.6
  225.5 0.0 copy-done.7
  225.5 1.6 convert_reduce_fusion.1
  227.1 0.4 convolution_reduce_fusion
  227.6 0.0 copy-start.9
  227.6 0.0 copy-start.10
  227.6 0.0 all-gather.2.cloned.1.call-done
  227.6 3.9 %fusion.24 = (f32[384]{0:T(512)S(1)}, f32[384]{0:T(512)S(1)}, f32[361,384]{1,0:T(8,128)S(1)}) fusion(bf16[2304,384]{1,0:T(8,128)(2,1)} %all-gather.2.cloned.1.call-done, f32[2304]{0:T(1024)S(1)} %add_divide_fusion, f32[2304]{0:T(1024)S(1)} %copy-done.6, f32[2304]{0:T(1024)S(1)} %copy-done.7, f32[2304]{0:T(1024)S(1)} %get-tuple-element.37, ...), kind=kOutput, calls=%fused_computation.106 | convolution fusion | flops 649452672 | bytes 5700096 | tf_op jit(solution)/shard_map/dot_general | solution.py:92
  231.6 0.1 broadcast_multiply_fusion.2
  231.7 30.0 %psum.23 = f32[2,2,384]{2,1,0:T(2,128)S(1)} all-reduce(f32[2,2,384]{2,1,0:T(2,128)S(1)} %broadcast_multiply_fusion.2), channel_id=1, replica_groups=mesh['grp'=2,'bn'=16] {'bn'}, use_global_device_ids=true, to_apply=%region_13.14 | all-reduce | flops 1536 | bytes 12288 | tf_op jit(solution)/shard_map/psum | solution.py:33
  261.6 0.1 multiply_reduce_fusion.4
  261.8 0.1 add_convert_fusion.1
  261.9 0.8 reshape.247
  (24 shorter events, 0.2 us)
Async XLA Ops:
  6.5 220.6 %copy-start = (bf16[96,2304]{1,0:T(8,128)(2,1)S(1)}, bf16[96,2304]{1,0:T(8,128)(2,1)}, u32[]{:S(2)}) copy-start(bf16[96,2304]{1,0:T(8,128)(2,1)} %param.24) | copy-start | bytes 1327108
  6.5 10.5 %copy-start.3 = (bf16[1,19,19,384]{3,2,1,0:T(8,128)(2,1)S(1)}, bf16[1,19,19,384]{3,2,1,0:T(8,128)(2,1)}, u32[]{:S(2)}) copy-start(bf16[1,19,19,384]{3,2,1,0:T(8,128)(2,1)} %param.15) | copy-start | bytes 831748
  6.5 10.6 %copy-start.12 = (s32[16]{0:T(128)S(1)}, s32[16]{0:T(128)}, u32[]{:S(2)}) copy-start(s32[16]{0:T(128)} %param.29) | copy-start | bytes 196
  6.5 13.8 %copy-start.2 = (bf16[25,2304]{1,0:T(8,128)(2,1)S(1)}, bf16[25,2304]{1,0:T(8,128)(2,1)}, u32[]{:S(2)}) copy-start(bf16[25,2304]{1,0:T(8,128)(2,1)} %param.19) | copy-start | bytes 345604
  8.9 46.2 %all-to-all-start = ((bf16[16,24,2304]{2,1,0:T(8,128)(2,1)}), bf16[16,24,2304]{2,1,0:T(8,128)(2,1)S(1)}, u32[]{:S(2)}, u32[]{:S(2)}) async-start(bf16[16,24,2304]{2,1,0:T(8,128)(2,1)} %stack.20), calls=%async_computation | async-start | bytes 3538944 | tf_op jit(solution)/shard_map/all_to_all | solution.py:70
  16.2 211.4 %all-gather.2.cloned.1.call-start = ((), (), s32[]{:S(2)}) async-start(), calls=%async_computation.1 | async-start | bytes 1880064 | tf_op jit(solution)/shard_map/all_gather | solution.py:94
  55.1 72.4 %copy-start.4 = (f32[2304]{0:T(1024)S(1)}, f32[2304]{0:T(1024)}, u32[]{:S(2)}) copy-start(f32[2304]{0:T(1024)} %param.18) | copy-start | bytes 27652
  55.1 72.4 %copy-start.5 = (f32[2304]{0:T(1024)S(1)}, f32[2304]{0:T(1024)}, u32[]{:S(2)}) copy-start(f32[2304]{0:T(1024)} %param.17) | copy-start | bytes 27652
  165.1 60.4 %copy-start.6 = (f32[2304]{0:T(1024)S(1)}, f32[2304]{0:T(1024)}, u32[]{:S(2)}) copy-start(f32[2304]{0:T(1024)} %param.21) | copy-start | bytes 27652
  165.1 60.4 %copy-start.7 = (f32[2304]{0:T(1024)S(1)}, f32[2304]{0:T(1024)}, u32[]{:S(2)}) copy-start(f32[2304]{0:T(1024)} %param.20) | copy-start | bytes 27652
  165.1 62.0 %copy-start.1 = (bf16[2304,96]{0,1:T(8,128)(2,1)S(1)}, bf16[2304,96]{0,1:T(8,128)(2,1)}, u32[]{:S(2)}) copy-start(bf16[2304,96]{0,1:T(8,128)(2,1)} %param.22) | copy-start | bytes 1327108
  165.1 62.0 %copy-start.11 = (f32[96]{0:T(128)S(1)}, f32[96]{0:T(128)}, u32[]{:S(2)}) copy-start(f32[96]{0:T(128)} %param.23) | copy-start | bytes 1156
  165.1 62.4 %copy-start.8 = (f32[2304]{0:T(1024)S(1)}, f32[2304]{0:T(1024)}, u32[]{:S(2)}) copy-start(f32[2304]{0:T(1024)} %param.25) | copy-start | bytes 27652
  227.6 34.2 %copy-start.9 = (f32[384]{0:T(512)S(1)}, f32[384]{0:T(512)}, u32[]{:S(2)}) copy-start(f32[384]{0:T(512)} %param.28) | copy-start | bytes 4612
  227.6 34.2 %copy-start.10 = (f32[384]{0:T(512)S(1)}, f32[384]{0:T(512)}, u32[]{:S(2)}) copy-start(f32[384]{0:T(512)} %param.27) | copy-start | bytes 4612
Sparse Core Ops, SparseCore 0:
  19.2 52.9 all-gather.1
